TPU v7x, 256 devices: a whole 4x4x8 slice. The times are simulated.
256 devices in a mesh: leaf: 256 (over x, y, z, core).
Axes of the slice: x: 4, y: 4, z: 8, core: 2. Of those that a mesh axis runs over, the one named last changes fastest.
Arguments:
- coarse_basis: float32 [9, 131072, 256], P(None, 'leaf'), as said below
- rhs_vectors_coarse: float32 [131072, 768], P('leaf'), may hold values from -6 to 6
- vertex_tier_depth: int32 [131072], P('leaf'), may hold values from 0 to 8
Outputs:
- solution: float32 [131072, 768], P('leaf')
Inputs may be any that keep to these rules, and one draw needn't show every extreme that they name: vertex_tier_depth[v] is the coarsest separator level whose block has vertex v in its support; level 0 is the vertex's own leaf block. `coarse_basis`: float32 entries, finite.
All inputs are finite; a program needn't handle non-finite values.
Results may differ from a plain program's by a relative error of at most 0.0001.
Values sent between devices are 32-bit elements; how exact they have to be, the bound alone decides.
A program may use at most 128 MiB of HBM per device.

v0:
```python
import functools

import jax
import jax.numpy as jnp
from jax import lax
from jax.experimental import pallas as pl
from jax.experimental.pallas import tpu as pltpu
from jax.sharding import PartitionSpec as P

MESH = pl.DeviceIdType.MESH
F32, BF16 = jnp.float32, jnp.bfloat16

S, V, R = 256, 512, 768
HALF = R // 2
NX, NY, NZ = 4, 4, 8
LEVELS = 9
RECV_ROWS, N_SEND, N_RECV = 6400, 128, 128

ORDER = [8, 4, 8, 7, 4, 5, 7, 8, 6, 4, 5, 3, 6, 7, 8, 4, 2, 5, 3, 6, 7, 8, 4, 2, 5, 1, 3, 6, 7, 8, 4, 0, 5, 1,
         3, 6, 7, 8, 4, 0, 2, 5, 3, 6, 7, 8, 4, 2, 5, 3, 6, 7, 8, 4, 5, 7, 8, 4, 5, 4, 5, 5, 5]


def split(x):
    hi = x.astype(BF16)
    return hi, (x - hi.astype(F32)).astype(BF16)


def aligned(offset, by=8):
    return offset if isinstance(offset, int) else pl.multiple_of(offset, by)


class Exchange:
    def __init__(self, part, coef, recv, send_sem, recv_sem, me):
        self.part, self.coef, self.recv = part, coef, recv
        self.send_sem, self.recv_sem, self.me = send_sem, recv_sem, me
        self.rows = self.sends = self.recvs = 0
        self.started = []

    def slots(self, n, rows):
        first, sem = self.rows, self.recvs
        self.rows += n * rows
        self.recvs += n
        assert self.rows <= RECV_ROWS and self.recvs <= N_RECV
        return first, sem

    def sems(self, n):
        sem = self.recvs
        self.recvs += n
        assert self.recvs <= N_RECV
        return sem

    def at(self, ref, level, offset, rows):
        offset = aligned(offset)
        return ref.at[pl.ds(offset, rows)] if level is None else ref.at[level, pl.ds(offset, rows)]

    def send(self, src, dst, sem, device, when=None):
        copy = pltpu.make_async_remote_copy(
            src_ref=src, dst_ref=dst, send_sem=self.send_sem.at[self.sends], recv_sem=self.recv_sem.at[sem],
            device_id=(device,), device_id_type=MESH)
        self.sends += 1
        assert self.sends <= N_SEND
        self.started.append((copy, when))
        if when is None:
            copy.start()
        else:
            pl.when(when)(copy.start)

    def wait(self, dst, sem, device):
        pltpu.make_async_remote_copy(
            src_ref=dst, dst_ref=dst, send_sem=self.send_sem.at[0], recv_sem=self.recv_sem.at[sem],
            device_id=(device,), device_id_type=MESH).wait_recv()

    def drain(self):
        for copy, when in self.started:
            if when is None:
                copy.wait_send()
            else:
                pl.when(when)(copy.wait_send)


def kernel(basis, rhs, depth, out, bas_v, rhs_v, x_hi, x_lo, b_hi, b_lo, tier, part, coef, recv, acc,
           load_sem, store_sem, send_sem, recv_sem):
    me = lax.axis_index("leaf")
    core = lax.rem(me, 2)
    z = lax.rem(me // 2, NZ)
    y = lax.rem(me // (2 * NZ), NY)
    x = me // (2 * NZ * NY)

    def at_core(c):
        return me - core + c

    def at_z(k):
        return me + 2 * (k - z)

    def at_y(k):
        return me + 2 * NZ * (k - y)

    def at_x(k):
        return me + 2 * NZ * NY * (k - x)

    barrier = pltpu.get_barrier_semaphore()
    partners = [at_core(1 - core)]
    partners += [at_z(lax.rem(z + d, NZ)) for d in range(1, NZ)]
    partners += [at_y(lax.rem(y + d, NY)) for d in range(1, NY)]
    partners += [at_x(lax.rem(x + d, NX)) for d in range(1, NX)]
    for partner in partners:
        pl.semaphore_signal(barrier, inc=1, device_id=(partner,), device_id_type=MESH)

    first_seen = list(dict.fromkeys(ORDER))
    load_rhs = pltpu.make_async_copy(rhs, rhs_v, load_sem.at[LEVELS])
    load_rhs.start()
    loads = {}
    for level in first_seen:
        loads[level] = pltpu.make_async_copy(basis.at[level], bas_v.at[level], load_sem.at[level])
        loads[level].start()

    for k in range(V // 128):
        row = depth[0:1, 128 * k:128 * (k + 1)].astype(F32)
        tier[128 * k:128 * (k + 1), :] = jnp.broadcast_to(row, (128, 128)).T

    load_rhs.wait()
    for k in range(R // 128):
        hi, lo = split(rhs_v[:, 128 * k:128 * (k + 1)].T)
        b_hi[128 * k:128 * (k + 1), :] = hi
        b_lo[128 * k:128 * (k + 1), :] = lo

    ex = Exchange(part, coef, recv, send_sem, recv_sem, me)
    mine = core * HALF

    def project(level):
        loads[level].wait()
        for k in range(S // 128):
            cols = slice(128 * k, 128 * (k + 1))
            kept = jnp.where(tier[...] >= float(level), bas_v[level, :, cols], 0.0)
            hi, lo = split(kept)
            x_hi[level, :, cols] = hi
            x_lo[level, :, cols] = lo
        hi, lo = x_hi[level], x_lo[level]
        part[level] = (jnp.dot(b_hi[...], hi, preferred_element_type=F32)
                       + jnp.dot(b_hi[...], lo, preferred_element_type=F32)
                       + jnp.dot(b_lo[...], hi, preferred_element_type=F32))

    def nt(a, b):
        return lax.dot_general(a, b, (((1,), (1,)), ((), ())), preferred_element_type=F32)

    state = {"applied": 0}
    stores = []

    def apply(level, coefficients):
        hi, lo = split(coefficients)
        first, last = state["applied"] == 0, state["applied"] == LEVELS - 1
        state["applied"] += 1
        if not last:
            image = nt(x_hi[level], hi) + nt(x_hi[level], lo) + nt(x_lo[level], hi)
            acc[...] = image if first else acc[...] + image
            return
        for k in range(4):
            rows = slice(k * V // 4, (k + 1) * V // 4)
            image = nt(x_hi[level, rows], hi) + nt(x_hi[level, rows], lo) + nt(x_lo[level, rows], hi)
            acc[rows, :] = acc[rows, :] + image
            stores.append(pltpu.make_async_copy(acc.at[rows], out.at[rows], store_sem.at[k]))
            stores[-1].start()

    def add_into(level, offset, rows, slots):
        where = pl.ds(aligned(offset), rows)
        total = part[level, where, :]
        for slot in slots:
            total = total + recv[pl.ds(slot, rows), :]
        part[level, where, :] = total

    def cores_in(level):
        first, sem = ex.slots(1, HALF)
        other = at_core(1 - core)
        ex.send(ex.at(part, level, HALF - mine, HALF), ex.at(recv, None, first, HALF), sem, other)
        yield
        ex.wait(ex.at(recv, None, first, HALF), sem, other)
        add_into(level, mine, HALF, [first])

    def cores_out(level):
        sem = ex.sems(1)
        other = at_core(1 - core)
        ex.send(ex.at(coef, level, mine, HALF), ex.at(coef, level, mine, HALF), sem, other)
        yield
        ex.wait(ex.at(coef, level, HALF - mine, HALF), sem, other)

    def pair_in(level, base, rows, bit, other):
        first, sem = ex.slots(1, rows)
        ex.send(ex.at(part, level, base + (1 - bit) * rows, rows), ex.at(recv, None, first, rows), sem, other)
        yield
        ex.wait(ex.at(recv, None, first, rows), sem, other)
        add_into(level, base + bit * rows, rows, [first])

    def pair_out(level, base, rows, bit, other):
        sem = ex.sems(1)
        block = ex.at(coef, level, base + bit * rows, rows)
        ex.send(block, block, sem, other)
        yield
        ex.wait(ex.at(coef, level, base + (1 - bit) * rows, rows), sem, other)

    def four_in(level, base, rows, pos, device):
        first, sem = ex.slots(3, rows)
        for d in range(1, 4):
            to = lax.rem(pos + d, 4)
            ex.send(ex.at(part, level, base + to * rows, rows), ex.at(recv, None, first + (d - 1) * rows, rows),
                    sem + d - 1, device(to))
        yield
        for d in range(1, 4):
            ex.wait(ex.at(recv, None, first + (d - 1) * rows, rows), sem + d - 1, device(lax.rem(pos + 4 - d, 4)))
        add_into(level, base + pos * rows, rows, [first + d * rows for d in range(3)])

    def four_out(level, base, rows, pos, device):
        sem = ex.sems(3)
        block = ex.at(coef, level, base + pos * rows, rows)
        for d in range(1, 4):
            ex.send(block, block, sem + d - 1, device(lax.rem(pos + d, 4)))
        yield
        for d in range(1, 4):
            source = lax.rem(pos + 4 - d, 4)
            ex.wait(ex.at(coef, level, base + source * rows, rows), sem + d - 1, device(source))

    def roots_sum(level, base, rows, count):
        if count == 3:
            places = [2 * r for r in range(3)]
            is_root, my_root = jnp.logical_and(lax.rem(z, 2) == 0, z < 6), z // 2
        else:
            places = [r + r // 3 for r in range(6)]
            is_root, my_root = lax.rem(z, 4) != 3, z - z // 4
        first, sem = ex.slots(NZ - 1, rows)
        for r, place in enumerate(places):
            slot = lax.rem(z - place + NZ, NZ) - 1
            slot = jnp.maximum(slot, 0)
            ex.send(ex.at(part, level, base + r * rows, rows), ex.at(recv, None, first + slot * rows, rows),
                    sem + slot, at_z(place), when=z != place)
        yield
        back = ex.sems(count)
        where = base + my_root * rows

        @pl.when(is_root)
        def _():
            for d in range(1, NZ):
                ex.wait(ex.at(recv, None, first + (d - 1) * rows, rows), sem + d - 1, at_z(lax.rem(z + d, NZ)))
            total = part[level, pl.ds(aligned(where), rows), :]
            for d in range(NZ - 1):
                total = total + recv[pl.ds(first + d * rows, rows), :]
            coef[level, pl.ds(aligned(where), rows), :] = total

        block = ex.at(coef, level, jnp.where(is_root, where, base), rows)
        sem_at = back + jnp.where(is_root, my_root, 0)
        for d in range(1, NZ):
            ex.send(block, block, sem_at, at_z(lax.rem(z + d, NZ)), when=is_root)
        yield
        for r, place in enumerate(places):
            @pl.when(z != place)
            def _():
                ex.wait(ex.at(coef, level, base + r * rows, rows), back + r, at_z(place))

    def chain_sum(level, base, rows):
        cut = rows // 16 * 8
        up, down = at_z(lax.rem(z + 1, NZ)), at_z(lax.rem(z + NZ - 1, NZ))

        def block(d):
            return base + lax.rem(z + d + NZ, NZ) * rows

        for step in range(1, 5):
            far = 5 - step
            n_up, n_down, skip = (cut, rows - cut, cut) if step == 1 else (rows, rows, 0)
            first, sem = ex.slots(1, n_up)
            first_down, sem_down = ex.slots(1, n_down)
            ex.send(ex.at(part, level, block(far), n_up), ex.at(recv, None, first, n_up), sem, up)
            ex.send(ex.at(part, level, block(-far) + skip, n_down), ex.at(recv, None, first_down, n_down), sem_down, down)
            yield
            ex.wait(ex.at(recv, None, first, n_up), sem, down)
            ex.wait(ex.at(recv, None, first_down, n_down), sem_down, up)
            if step < 4:
                add_into(level, block(far - 1), n_up, [first])
                add_into(level, block(1 - far) + skip, n_down, [first_down])
        own = pl.ds(aligned(block(0)), rows)
        coef[level, own, :] = part[level, own, :] + recv[pl.ds(first, rows), :] + recv[pl.ds(first_down, rows), :]
        for step in range(1, 5):
            n_up, n_down, skip = (cut, rows - cut, cut) if step == 4 else (rows, rows, 0)
            sem = ex.sems(2)
            going_up = ex.at(coef, level, block(1 - step), n_up)
            going_down = ex.at(coef, level, block(step - 1) + skip, n_down)
            ex.send(going_up, going_up, sem, up)
            ex.send(going_down, going_down, sem + 1, down)
            yield
            ex.wait(ex.at(coef, level, block(-step), n_up), sem, down)
            ex.wait(ex.at(coef, level, block(step) + skip, n_down), sem + 1, up)

    def quad_sum(level, base):
        rows = HALF // 2
        place = lax.rem(z, 4)
        side = place // 2
        start = z - place
        middle = jnp.logical_or(place == 1, place == 2)
        edge = jnp.logical_not(middle)
        my_middle, my_edge, far_middle = at_z(start + 1 + side), at_z(start + 3 * side), at_z(start + 2 - side)
        near, far = base + side * rows, base + (1 - side) * rows
        first, sem = ex.slots(3, rows)
        back = ex.sems(2)
        slot = [ex.at(recv, None, first + k * rows, rows) for k in range(3)]
        ex.send(ex.at(part, level, far, rows), slot[0], sem, my_middle, when=edge)
        ex.send(ex.at(part, level, near, rows), slot[1], sem + 1, my_middle, when=edge)
        yield

        @pl.when(middle)
        def _():
            ex.wait(slot[0], sem, my_edge)
            add_into(level, far, rows, [first])

        ex.send(ex.at(part, level, far, rows), slot[2], sem + 2, far_middle, when=middle)
        yield

        @pl.when(middle)
        def _():
            ex.wait(slot[1], sem + 1, my_edge)
            ex.wait(slot[2], sem + 2, far_middle)
            where = pl.ds(aligned(near), rows)
            coef[level, where, :] = (part[level, where, :] + recv[pl.ds(first + rows, rows), :]
                                     + recv[pl.ds(first + 2 * rows, rows), :])

        block, other = ex.at(coef, level, near, rows), ex.at(coef, level, far, rows)
        ex.send(block, block, back, far_middle, when=middle)
        ex.send(block, block, back + 1, my_edge, when=middle)
        yield

        @pl.when(middle)
        def _():
            ex.wait(other, back, far_middle)

        ex.send(other, other, back, my_edge, when=middle)
        yield

        @pl.when(edge)
        def _():
            ex.wait(block, back + 1, my_middle)
            ex.wait(other, back, my_middle)

    def level_0():
        project(0)
        yield
        apply(0, part[0])

    def level_1():
        project(1)
        first, sem = ex.slots(1, R)
        other = at_core(1 - core)
        ex.send(part.at[1], ex.at(recv, None, first, R), sem, other)
        yield
        ex.wait(ex.at(recv, None, first, R), sem, other)
        apply(1, part[1] + recv[pl.ds(first, R), :])

    def level_2():
        project(2)
        yield from cores_in(2)
        first, sem = ex.slots(1, HALF)
        other = at_z(z + 1 - 2 * lax.rem(z, 2))
        ex.send(ex.at(part, 2, mine, HALF), ex.at(recv, None, first, HALF), sem, other)
        yield
        ex.wait(ex.at(recv, None, first, HALF), sem, other)
        own = pl.ds(aligned(mine), HALF)
        coef[2, own, :] = part[2, own, :] + recv[pl.ds(first, HALF), :]
        yield from cores_out(2)
        apply(2, coef[2])

    def level_3():
        project(3)
        yield from cores_in(3)
        yield from quad_sum(3, mine)
        yield from cores_out(3)
        apply(3, coef[3])

    def level_4():
        project(4)
        yield from cores_in(4)
        yield from chain_sum(4, mine, HALF // 8)
        yield from cores_out(4)
        apply(4, coef[4])

    def level_5():
        project(5)
        yield from cores_in(5)
        bit = lax.rem(y, 2)
        other = at_y(y + 1 - 2 * bit)
        yield from pair_in(5, mine, HALF // 2, bit, other)
        yield from chain_sum(5, mine + bit * (HALF // 2), HALF // 16)
        yield from pair_out(5, mine, HALF // 2, bit, other)
        yield from cores_out(5)
        apply(5, coef[5])

    def level_6():
        project(6)
        yield from cores_in(6)
        yield from four_in(6, mine, HALF // 4, y, at_y)
        yield from roots_sum(6, mine + y * (HALF // 4), HALF // 24, 6)
        yield from four_out(6, mine, HALF // 4, y, at_y)
        yield from cores_out(6)
        apply(6, coef[6])

    def level_7():
        project(7)
        yield from cores_in(7)
        bit = lax.rem(x, 2)
        other = at_x(x + 1 - 2 * bit)
        yield from pair_in(7, mine, HALF // 2, bit, other)
        base = mine + bit * (HALF // 2)
        yield from four_in(7, base, HALF // 8, y, at_y)
        yield from roots_sum(7, base + y * (HALF // 8), HALF // 48, 6)
        yield from four_out(7, base, HALF // 8, y, at_y)
        yield from pair_out(7, mine, HALF // 2, bit, other)
        yield from cores_out(7)
        apply(7, coef[7])

    def level_8():
        project(8)
        yield from cores_in(8)
        yield from four_in(8, mine, HALF // 4, x, at_x)
        base = mine + x * (HALF // 4)
        yield from four_in(8, base, HALF // 16, y, at_y)
        yield from roots_sum(8, base + y * (HALF // 16), HALF // 48, 3)
        yield from four_out(8, base, HALF // 16, y, at_y)
        yield from four_out(8, mine, HALF // 4, x, at_x)
        yield from cores_out(8)
        apply(8, coef[8])

    pl.semaphore_wait(barrier, len(partners))
    levels = [f() for f in (level_0, level_1, level_2, level_3, level_4, level_5, level_6, level_7, level_8)]
    for level in ORDER:
        next(levels[level], None)
    for level in (1, 2, 3, 6, 7, 8, 4, 5):
        for _ in levels[level]:
            pass
    assert state["applied"] == LEVELS
    ex.drain()
    for store in stores:
        store.wait()


def body(basis, rhs, depth):
    any_space = pl.BlockSpec(memory_space=pl.ANY)
    return pl.pallas_call(
        kernel,
        out_shape=jax.ShapeDtypeStruct((V, R), F32),
        in_specs=[any_space, any_space, pl.BlockSpec(memory_space=pltpu.VMEM)],
        out_specs=any_space,
        scratch_shapes=[
            pltpu.VMEM((LEVELS, V, S), F32),
            pltpu.VMEM((V, R), F32),
            pltpu.VMEM((LEVELS, V, S), BF16),
            pltpu.VMEM((LEVELS, V, S), BF16),
            pltpu.VMEM((R, V), BF16),
            pltpu.VMEM((R, V), BF16),
            pltpu.VMEM((V, 128), F32),
            pltpu.VMEM((LEVELS, R, S), F32),
            pltpu.VMEM((LEVELS, R, S), F32),
            pltpu.VMEM((RECV_ROWS, S), F32),
            pltpu.VMEM((V, R), F32),
            pltpu.SemaphoreType.DMA((LEVELS + 1,)),
            pltpu.SemaphoreType.DMA((4,)),
            pltpu.SemaphoreType.DMA((N_SEND,)),
            pltpu.SemaphoreType.DMA((N_RECV,)),
        ],
        compiler_params=pltpu.CompilerParams(
            collective_id=0, has_side_effects=True, vmem_limit_bytes=60 * 1024 * 1024),
        name="coarse_solve",
    )(basis, rhs, depth.reshape(1, V))


def solution(mesh):
    in_specs = (P(None, "leaf", None), P("leaf", None), P("leaf"))
    out_specs = P("leaf", None)
    return jax.shard_map(body, mesh=mesh, in_specs=in_specs, out_specs=out_specs, check_vma=False)
```

profile of v0, /device:TPU:1, one launch (start us, length us, event | category | flops | bytes accessed | tf_op | source)
XLA Modules:
  0.0 94.7 jit_solution(397909750450497483)
XLA Ops:
  0.0 92.0 %coarse_solve.1 = f32[512,768]{1,0:T(8,128)} custom-call(f32[9,512,256]{2,1,0:T(8,128)} %basis.1, f32[512,768]{1,0:T(8,128)} %rhs.1, s32[1,512]{1,0:T(1,128)} %bitcast.1), custom_call_target="tpu_custom_call" | custom-call | tf_op jit(solution)/shard_map/coarse_solve/pallas_call | solution.py:441
  92.0 2.7 %copy.5 = f32[512,768]{1,0:T(8,128)} copy(f32[512,768]{1,0:T(8,128)} %coarse_solve.1) | data formatting | bytes 3145728
where the time goes:
time: 95 us; the launch traced here: 94.7 us
  Pallas kernels  92 us (97%)
  local copies, waits for them, and re-layouts  2.65 us (3%)
    pallas_call x1, Pallas kernels, body(): pl.pallas_call(kernel, out_shape=jax.ShapeDtypeStruct((V, R), F32), in_sp...  92 us
    unnamed x1, local copies, waits for them, and re-layouts  2.65 us

commit v1 on v0

v1 whole, which is shorter than its diff:
```python
import functools

import jax
import jax.numpy as jnp
from jax import lax
from jax.experimental import pallas as pl
from jax.experimental.pallas import tpu as pltpu
from jax.sharding import PartitionSpec as P

MESH = pl.DeviceIdType.MESH
F32, BF16 = jnp.float32, jnp.bfloat16

S, V, R = 256, 512, 768
HALF = R // 2
NX, NY, NZ = 4, 4, 8
LEVELS = 9
EARLY = 4
RECV_ROWS, N_SEND, N_RECV = 6400, 16, 112

ORDER = [5, 4, 7, 3, 6, 8, 5, 4, 1, 3, 30, 7, 2, 6, 4, 8, 5, 2, 6, 30, 23, 7, 5, 8, 4, 6, 20, 7, 5, 8, 6, 1, 7, 6, 5,
         8, 4, 8, 20, 6, 7, 6, 4, 0, 5, 8, 6, 31, 30, 7, 5, 6, 21, 7, 30, 8, 31, 6, 8, 4, 5, 7, 31, 6, 21, 0, 8, 5, 4,
         6, 31, 5, 30, 23, 8, 4, 22, 7, 6, 31, 7, 4, 6, 8, 3, 22, 5, 4, 8, 2, 5]


def split(x):
    hi = x.astype(BF16)
    return hi, (x - hi.astype(F32)).astype(BF16)


def aligned(offset, by=8):
    return offset if isinstance(offset, int) else pl.multiple_of(offset, by)


class Exchange:
    def __init__(self, recv, send_sem, recv_sem, other):
        self.recv, self.send_sem, self.recv_sem, self.other = recv, send_sem, recv_sem, other
        self.rows = self.sends = self.recvs = 0
        self.sent = {}

    def slots(self, rows):
        first = self.rows
        self.rows += rows
        assert self.rows <= RECV_ROWS
        return first

    def sem(self):
        self.recvs += 1
        assert self.recvs <= N_RECV
        return self.recv_sem.at[self.recvs - 1]

    def at(self, ref, level, offset, rows, cols=None):
        where = (pl.ds(aligned(offset), rows),)
        if cols is not None:
            where += (pl.ds(aligned(cols, 128), 128),)
        return ref.at[where] if level is None else ref.at[(level,) + where]

    def group(self, key):
        if key not in self.sent:
            assert self.sends < N_SEND
            self.sent[key] = [self.send_sem.at[self.sends], 0, None]
            self.sends += 1
        return self.sent[key]

    def send(self, src, dst, sem, device, key, when=None, drain=True):
        group = self.group(key)
        copy = pltpu.make_async_remote_copy(
            src_ref=src, dst_ref=dst, send_sem=group[0], recv_sem=sem, device_id=(device,), device_id_type=MESH)
        if drain:
            group[1] += src.shape[0] * src.shape[1] // 128
            group[2] = when
        if when is None:
            copy.start()
        else:
            pl.when(when)(copy.start)

    def whole(self, halves):
        if halves % 16:
            return self.recv.at[pl.ds(0, halves), pl.ds(0, 128)]
        return self.recv.at[pl.ds(0, halves // 2)]

    def descriptor(self, halves, send_sem, recv_sem):
        ref = self.whole(halves)
        return pltpu.make_async_remote_copy(
            src_ref=ref, dst_ref=ref, send_sem=send_sem, recv_sem=recv_sem, device_id=(self.other,),
            device_id_type=MESH)

    def wait(self, rows, sem, narrow=False):
        self.descriptor(rows if narrow else 2 * rows, self.send_sem.at[0], sem).wait_recv()

    def wait_sent(self, rows, sem):
        self.descriptor(2 * rows, sem, self.recv_sem.at[0]).wait_send()

    def drain(self):
        for sem, halves, when in self.sent.values():
            if halves:
                wait = self.descriptor(halves, sem, self.recv_sem.at[0]).wait_send
                wait() if when is None else pl.when(when)(wait)


def kernel(basis, rhs, depth, out, bas_v, rhs_v, x_hi, x_lo, b_hi, b_lo, tier, part, coef, recv, acc,
           load_sem, send_sem, recv_sem):
    me = lax.axis_index("leaf")
    core = lax.rem(me, 2)
    z = lax.rem(me // 2, NZ)
    y = lax.rem(me // (2 * NZ), NY)
    x = me // (2 * NZ * NY)

    def at_core(c):
        return me - core + c

    def at_z(k):
        return me + 2 * (k - z)

    def at_y(k):
        return me + 2 * NZ * (k - y)

    def at_x(k):
        return me + 2 * NZ * NY * (k - x)

    barrier = pltpu.get_barrier_semaphore()
    partners = [at_core(1 - core)]
    partners += [at_z(lax.rem(z + d, NZ)) for d in range(1, NZ)]
    partners += [at_y(lax.rem(y + d, NY)) for d in range(1, NY)]
    partners += [at_x(lax.rem(x + d, NX)) for d in range(1, NX)]
    for partner in partners:
        pl.semaphore_signal(barrier, inc=1, device_id=(partner,), device_id_type=MESH)

    first_seen = [level for level in dict.fromkeys(ORDER) if level < LEVELS]
    load_rhs = pltpu.make_async_copy(rhs, rhs_v, load_sem.at[LEVELS])
    load_rhs.start()
    loads = {}
    for level in first_seen:
        loads[level] = pltpu.make_async_copy(basis.at[level], bas_v.at[level], load_sem.at[level])
        loads[level].start()

    for k in range(V // 128):
        row = depth[0:1, 128 * k:128 * (k + 1)].astype(F32)
        tier[128 * k:128 * (k + 1), :] = jnp.broadcast_to(row, (128, 128)).T

    load_rhs.wait()
    for k in range(R // 128):
        hi, lo = split(rhs_v[:, 128 * k:128 * (k + 1)].T)
        b_hi[128 * k:128 * (k + 1), :] = hi
        b_lo[128 * k:128 * (k + 1), :] = lo

    ex = Exchange(recv, send_sem, recv_sem, at_core(1 - core))
    mine = core * HALF

    projected, prepared = set(), set()

    def prepare(level):
        if level in prepared:
            return
        prepared.add(level)
        loads[level].wait()
        for k in range(S // 128):
            cols = slice(128 * k, 128 * (k + 1))
            kept = jnp.where(tier[...] >= float(level), bas_v[level, :, cols], 0.0)
            hi, lo = split(kept)
            x_hi[level, :, cols] = hi
            x_lo[level, :, cols] = lo

    def project(level):
        if level in projected:
            return
        projected.add(level)
        prepare(level)
        if len(projected) < LEVELS:
            prepare(first_seen[len(projected)])
        for k in range(2):
            rows = slice(k * HALF, (k + 1) * HALF)
            hi, lo = x_hi[level], x_lo[level]
            part[level, rows] = (jnp.dot(b_hi[rows], hi, preferred_element_type=F32)
                                 + jnp.dot(b_hi[rows], lo, preferred_element_type=F32)
                                 + jnp.dot(b_lo[rows], hi, preferred_element_type=F32))

    def nt(a, b):
        return lax.dot_general(a, b, (((1,), (1,)), ((), ())), preferred_element_type=F32)

    state = {"applied": 0}

    tiles = [(0, V, 0), (0, V, 256), (0, V // 2, 512), (V // 2, V // 2, 512)]

    def apply(level, coefficients):
        first, last = state["applied"] == 0, state["applied"] == LEVELS - 1
        state["applied"] += 1
        for k, (row, rows, col) in enumerate(tiles):
            rows, cols = slice(row, row + rows), slice(col, col + 256)
            hi, lo = split(coefficients(cols))
            image = nt(x_hi[level, rows], hi) + nt(x_hi[level, rows], lo) + nt(x_lo[level, rows], hi)
            if last:
                out[rows, cols] = acc[rows, cols] + image
            else:
                acc[rows, cols] = image if first else acc[rows, cols] + image

    def add_into(level, offset, rows, slots):
        where = pl.ds(aligned(offset), rows)
        total = part[level, where, :]
        for slot in slots:
            total = total + recv[pl.ds(slot, rows), :]
        part[level, where, :] = total

    def cores_in(level):
        first, sem = ex.slots(HALF), ex.sem()
        ex.send(ex.at(part, level, HALF - mine, HALF), ex.at(recv, None, first, HALF), sem, ex.other, level)
        yield
        ex.wait(HALF, sem)
        add_into(level, mine, HALF, [first])

    def cores_out(level, sem, offset=0, rows=HALF):
        block = ex.at(coef, level, mine + offset, rows)
        ex.send(block, block, sem, ex.other, level)

    def both_cores(level):
        sem = ex.sem()
        cores_out(level, sem)
        yield
        ex.wait(HALF, sem)

    def pair_in(level, base, rows, bit, other):
        first, sem = ex.slots(rows), ex.sem()
        ex.send(ex.at(part, level, base + (1 - bit) * rows, rows), ex.at(recv, None, first, rows), sem, other, level)
        yield
        ex.wait(rows, sem)
        add_into(level, base + bit * rows, rows, [first])

    def pair_out(level, base, rows, bit, other):
        sem = ex.sem()
        block = ex.at(coef, level, base + bit * rows, rows)
        ex.send(block, block, sem, other, level)
        yield
        ex.wait(rows, sem)

    def roots_sum(level, base, rows, count):
        if count == 3:
            places = [2 * r for r in range(3)]
            is_root, my_root = jnp.logical_and(lax.rem(z, 2) == 0, z < 6), z // 2
        else:
            places = [r + r // 3 for r in range(6)]
            is_root, my_root = lax.rem(z, 4) != 3, z - z // 4
        not_root = jnp.logical_not(is_root)
        first, sem, back = ex.slots((NZ - 1) * rows), ex.sem(), ex.sem()
        for r, place in enumerate(places):
            slot = jnp.maximum(lax.rem(z - place + NZ, NZ) - 1, 0)
            ex.send(ex.at(part, level, base + r * rows, rows), ex.at(recv, None, first + slot * rows, rows),
                    sem, at_z(place), (level, "in"), when=z != place, drain=False)
        yield
        where = base + jnp.where(is_root, my_root * rows, 0)

        @pl.when(is_root)
        def _():
            ex.wait((NZ - 1) * rows, sem)
            total = part[level, pl.ds(aligned(where), rows), :]
            for d in range(NZ - 1):
                total = total + recv[pl.ds(first + d * rows, rows), :]
            coef[level, pl.ds(aligned(where), rows), :] = total

        block = ex.at(coef, level, where, rows)
        for d in range(1, NZ):
            ex.send(block, block, back, at_z(lax.rem(z + d, NZ)), (level, "out"), when=is_root)
        yield
        sent = ex.group((level, "in"))[0]

        @pl.when(is_root)
        def _():
            ex.wait((count - 1) * rows, back)
            ex.wait_sent((count - 1) * rows, sent)

        @pl.when(not_root)
        def _():
            ex.wait(count * rows, back)
            ex.wait_sent(count * rows, sent)

    def ring_blocks(level, base, rows, n, pos, narrow):
        def block(ref, lev, d, skip, size):
            k = lax.rem(pos + d + n, n)
            if narrow:
                return ex.at(ref, lev, base + (k // 2) * rows + skip, size, lax.rem(k, 2) * 128)
            return ex.at(ref, lev, base + k * rows + skip, size)

        return block

    def chain_in(level, base, rows, n, pos, device, total, narrow=False):
        cut = rows // 16 * 8
        up, down = device(lax.rem(pos + 1, n)), device(lax.rem(pos + n - 1, n))
        block = ring_blocks(level, base, rows, n, pos, narrow)
        cols = 0 if narrow else None
        last_down, last_up, last_sem = ex.slots(rows), ex.slots(rows), ex.sem()
        for far in range(n // 2, 0, -1):
            n_up, n_down, skip = (cut, rows - cut, cut) if far == n // 2 else (rows, rows, 0)
            first, first_down, sem = last_down, last_up, last_sem
            if far > 1:
                first, first_down, sem = ex.slots(n_up), ex.slots(n_down), ex.sem()
            elif n == 4:
                n_up, n_down, skip = cut, rows - cut, cut
            from_down, from_up = ex.at(recv, None, first, n_up, cols), ex.at(recv, None, first_down, n_down, cols)
            if n == 4 and far == 1:
                from_up = ex.at(recv, None, first_down + skip, n_down, cols)
            ex.send(block(part, level, far, 0, n_up), from_down, sem, up, level)
            ex.send(block(part, level, -far, skip, n_down), from_up, sem, down, level)
            if n == 4 and far == 2:
                ex.send(block(part, level, 1, cut, rows - cut), ex.at(recv, None, last_down + cut, rows - cut, cols),
                        last_sem, up, level)
                ex.send(block(part, level, -1, 0, cut), ex.at(recv, None, last_up, cut, cols), last_sem, down, level)
            yield
            if far > 1:
                ex.wait(n_up + n_down, sem, narrow)
                own = block(part, level, far - 1, 0, n_up)
                own[...] = own[...] + from_down[...]
                own = block(part, level, 1 - far, skip, n_down)
                own[...] = own[...] + from_up[...]
        ex.wait(2 * rows, last_sem, narrow)
        from_down, from_up = ex.at(recv, None, last_down, rows, cols), ex.at(recv, None, last_up, rows, cols)
        block(total, level, 0, 0, rows)[...] = block(part, level, 0, 0, rows)[...] + from_down[...] + from_up[...]

    def chain_out(level, base, rows, n, pos, device, narrow=False):
        cut = rows // 16 * 8
        up, down = device(lax.rem(pos + 1, n)), device(lax.rem(pos + n - 1, n))
        block = ring_blocks(level, base, rows, n, pos, narrow)

        def send(d, skip, size, sem, to):
            piece = block(coef, level, d, skip, size)
            ex.send(piece, piece, sem, to, level)

        if n == 4:
            sem, last_sem = ex.sem(), ex.sem()
            send(0, 0, cut, sem, up)
            send(0, cut, rows - cut, sem, down)
            send(0, cut, rows - cut, last_sem, up)
            send(0, 0, cut, last_sem, down)
            yield
            ex.wait(rows, sem, narrow)
            send(-1, 0, cut, last_sem, up)
            send(1, cut, rows - cut, last_sem, down)
            yield
            ex.wait(2 * rows, last_sem, narrow)
            return
        for far in range(1, n // 2 + 1):
            n_up, n_down, skip = (cut, rows - cut, cut) if far == n // 2 else (rows, rows, 0)
            sem = ex.sem()
            send(1 - far, 0, n_up, sem, up)
            send(far - 1, skip, n_down, sem, down)
            yield
            ex.wait(n_up + n_down, sem, narrow)

    def quad_sum(level, base, rows):
        place = lax.rem(z, 4)
        side = place // 2
        start = z - place
        middle = jnp.logical_or(place == 1, place == 2)
        edge = jnp.logical_not(middle)
        my_middle, my_edge, far_middle = at_z(start + 1 + side), at_z(start + 3 * side), at_z(start + 2 - side)
        near, far = base + side * rows, base + (1 - side) * rows
        first, sems = ex.slots(3 * rows), [ex.sem() for _ in range(3)]
        slot = [ex.at(recv, None, first + k * rows, rows) for k in range(3)]
        ex.send(ex.at(part, level, far, rows), slot[0], sems[0], my_middle, (level, "edge"), when=edge)
        ex.send(ex.at(part, level, near, rows), slot[1], sems[1], my_middle, (level, "edge"), when=edge)
        yield

        @pl.when(middle)
        def _():
            ex.wait(rows, sems[0])
            add_into(level, far, rows, [first])

        ex.send(ex.at(part, level, far, rows), slot[2], sems[1], far_middle, (level, "middle"), when=middle)
        yield

        @pl.when(middle)
        def _():
            ex.wait(2 * rows, sems[1])
            where = pl.ds(aligned(near), rows)
            coef[level, where, :] = (part[level, where, :] + recv[pl.ds(first + rows, rows), :]
                                     + recv[pl.ds(first + 2 * rows, rows), :])

        block, other = ex.at(coef, level, near, rows), ex.at(coef, level, far, rows)
        ex.send(block, block, sems[2], far_middle, (level, "middle"), when=middle)
        ex.send(block, block, sems[2], my_edge, (level, "middle"), when=middle)
        yield

        @pl.when(middle)
        def _():
            ex.wait(rows, sems[2])

        ex.send(other, other, sems[2], my_edge, (level, "middle"), when=middle)
        yield

        @pl.when(edge)
        def _():
            ex.wait(2 * rows, sems[2])

    def level_0():
        project(0)
        yield
        apply(0, lambda rows: part[0, rows])

    def level_1():
        project(1)
        first, sem = ex.slots(R), ex.sem()
        ex.send(part.at[1], ex.at(recv, None, first, R), sem, ex.other, 1)
        yield
        ex.wait(R, sem)
        apply(1, lambda rows: part[1, rows] + recv[first + rows.start:first + rows.stop, :])

    arrived = {2: ex.sem(), 3: ex.sem()}

    def level_2():
        project(2)
        yield from cores_in(2)
        yield
        ex.wait(HALF, arrived[2])
        apply(2, lambda rows: coef[2, rows])

    def chunk_2(k):
        rows = HALF // 4
        first, sem = ex.slots(rows), ex.sem()
        other = at_z(z + 1 - 2 * lax.rem(z, 2))
        ex.send(ex.at(part, 2, mine + k * rows, rows), ex.at(recv, None, first, rows), sem, other, 2)
        yield
        ex.wait(rows, sem)
        own = pl.ds(aligned(mine + k * rows), rows)
        coef[2, own, :] = part[2, own, :] + recv[pl.ds(first, rows), :]
        cores_out(2, arrived[2], k * rows, rows)

    def level_3():
        project(3)
        yield from cores_in(3)
        yield
        ex.wait(HALF, arrived[3])
        apply(3, lambda rows: coef[3, rows])

    def chunk_3(k):
        rows = HALF // 2
        yield from quad_sum(3, mine + k * rows, rows // 2)
        cores_out(3, arrived[3], k * rows, rows)

    def level_4():
        project(4)
        yield from cores_in(4)
        yield from chain_in(4, mine, HALF // NZ, NZ, z, at_z, coef)
        yield from chain_out(4, mine, HALF // NZ, NZ, z, at_z)
        yield from both_cores(4)
        apply(4, lambda rows: coef[4, rows])

    def level_5():
        project(5)
        yield from cores_in(5)
        bit = lax.rem(y, 2)
        other = at_y(y + 1 - 2 * bit)
        yield from pair_in(5, mine, HALF // 2, bit, other)
        base, rows = mine + bit * (HALF // 2), HALF // 2 // NZ
        yield from chain_in(5, base, rows, NZ, z, at_z, coef)
        yield from chain_out(5, base, rows, NZ, z, at_z)
        yield from pair_out(5, mine, HALF // 2, bit, other)
        yield from both_cores(5)
        apply(5, lambda rows: coef[5, rows])

    def level_6():
        project(6)
        yield from cores_in(6)
        yield from chain_in(6, mine, HALF // NY, NY, y, at_y, part)
        base, rows = mine + y * (HALF // NY), HALF // NY // NZ * 2
        yield from chain_in(6, base, rows, NZ, z, at_z, coef, narrow=True)
        yield from chain_out(6, base, rows, NZ, z, at_z, narrow=True)
        yield from chain_out(6, mine, HALF // NY, NY, y, at_y)
        yield from both_cores(6)
        apply(6, lambda rows: coef[6, rows])

    def level_7():
        project(7)
        yield from cores_in(7)
        bit = lax.rem(x, 2)
        other = at_x(x + 1 - 2 * bit)
        yield from pair_in(7, mine, HALF // 2, bit, other)
        base, rows = mine + bit * (HALF // 2), HALF // 2 // NY
        yield from chain_in(7, base, rows, NY, y, at_y, part)
        yield from roots_sum(7, base + y * rows, rows // 6, 6)
        yield from chain_out(7, base, rows, NY, y, at_y)
        yield from pair_out(7, mine, HALF // 2, bit, other)
        yield from both_cores(7)
        apply(7, lambda rows: coef[7, rows])

    def level_8():
        project(8)
        yield from cores_in(8)
        yield from chain_in(8, mine, HALF // NX, NX, x, at_x, part)
        base, rows = mine + x * (HALF // NX), HALF // NX // NY
        yield from chain_in(8, base, rows, NY, y, at_y, part)
        yield from roots_sum(8, base + y * rows, rows // 3, 3)
        yield from chain_out(8, base, rows, NY, y, at_y)
        yield from chain_out(8, mine, HALF // NX, NX, x, at_x)
        yield from both_cores(8)
        apply(8, lambda rows: coef[8, rows])

    levels = dict(enumerate(
        f() for f in (level_0, level_1, level_2, level_3, level_4, level_5, level_6, level_7, level_8)))
    levels.update({20 + k: chunk_2(k) for k in range(4)})
    levels.update({30 + k: chunk_3(k) for k in range(2)})
    early = first_seen[:EARLY]
    for level in early:
        project(level)
    pl.semaphore_wait(barrier, len(partners))
    for level in ORDER:
        next(levels[level], None)
    for rest in levels.values():
        for _ in rest:
            assert False
    assert state["applied"] == LEVELS
    ex.drain()


def body(basis, rhs, depth):
    hbm = pl.BlockSpec(memory_space=pltpu.HBM)
    return pl.pallas_call(
        kernel,
        out_shape=jax.ShapeDtypeStruct((V, R), F32),
        in_specs=[hbm, hbm, pl.BlockSpec(memory_space=pltpu.VMEM)],
        out_specs=pl.BlockSpec(memory_space=pltpu.VMEM),
        scratch_shapes=[
            pltpu.VMEM((LEVELS, V, S), F32),
            pltpu.VMEM((V, R), F32),
            pltpu.VMEM((LEVELS, V, S), BF16),
            pltpu.VMEM((LEVELS, V, S), BF16),
            pltpu.VMEM((R, V), BF16),
            pltpu.VMEM((R, V), BF16),
            pltpu.VMEM((V, 128), F32),
            pltpu.VMEM((LEVELS, R, S), F32),
            pltpu.VMEM((LEVELS, R, S), F32),
            pltpu.VMEM((RECV_ROWS, S), F32),
            pltpu.VMEM((V, R), F32),
            pltpu.SemaphoreType.DMA((LEVELS + 1,)),
            pltpu.SemaphoreType.DMA((N_SEND,)),
            pltpu.SemaphoreType.DMA((N_RECV,)),
        ],
        compiler_params=pltpu.CompilerParams(
            collective_id=0, has_side_effects=True, vmem_limit_bytes=52 * 1024 * 1024),
        name="coarse_solve",
    )(basis, rhs, depth.reshape(1, V))


def solution(mesh):
    in_specs = (P(None, "leaf", None), P("leaf", None), P("leaf"))
    out_specs = P("leaf", None)
    return jax.shard_map(body, mesh=mesh, in_specs=in_specs, out_specs=out_specs, check_vma=False)
```

time: 95 us -> 69.3 us (0.73)
  Pallas kernels: 92 us -> 67.4 us
    pallas_call x1, Pallas kernels: 92 us -> 67.4 us  [body(): pl.pallas_call(kernel, out_shape=jax.ShapeDtypeStruct((V, R), F32), in_sp...]
    unnamed x1 -> x3, local copies, waits for them, and re-layouts: 2.65 us -> 1.83 us
where the time goes in v1:
time: 69.3 us; the launch traced here: 69.2 us
  Pallas kernels  67.4 us (97%)
  local copies, waits for them, and re-layouts  1.83 us (3%)
    pallas_call x1, Pallas kernels, body(): pl.pallas_call(kernel, out_shape=jax.ShapeDtypeStruct((V, R), F32), in_sp...  67.4 us
    unnamed x3, local copies, waits for them, and re-layouts  1.83 us

profile of v1, /device:TPU:1, one launch (start us, length us, event | category | flops | bytes accessed | tf_op | source)
XLA Modules:
  0.0 69.2 jit_solution(17830556356929532751)
XLA Ops:
  0.0 0.0 copy-start
  0.0 0.7 copy-done
  0.7 67.4 %coarse_solve.1 = f32[512,768]{1,0:T(8,128)S(1)} custom-call(f32[9,512,256]{2,1,0:T(8,128)} %basis.1, f32[512,768]{1,0:T(8,128)} %rhs.1, s32[1,512]{1,0:T(1,128)S(1)} %bitcast.1), custom_call_target="tpu_custom_call" | custom-call | tf_op jit(solution)/shard_map/coarse_solve/pallas_call | solution.py:513
  68.1 1.1 %copy.5 = f32[512,768]{1,0:T(8,128)} copy(f32[512,768]{1,0:T(8,128)S(1)} %coarse_solve.1) | data formatting | bytes 3145728
Async XLA Ops:
  0.0 0.7 copy-start

commit v2 on v1

--- a/solution.py
+++ b/solution.py
@@ -14,12 +14,12 @@
 HALF = R // 2
 NX, NY, NZ = 4, 4, 8
 LEVELS = 9
-EARLY = 4
-RECV_ROWS, N_SEND, N_RECV = 6400, 16, 112
-
-ORDER = [5, 4, 7, 3, 6, 8, 5, 4, 1, 3, 30, 7, 2, 6, 4, 8, 5, 2, 6, 30, 23, 7, 5, 8, 4, 6, 20, 7, 5, 8, 6, 1, 7, 6, 5,
-         8, 4, 8, 20, 6, 7, 6, 4, 0, 5, 8, 6, 31, 30, 7, 5, 6, 21, 7, 30, 8, 31, 6, 8, 4, 5, 7, 31, 6, 21, 0, 8, 5, 4,
-         6, 31, 5, 30, 23, 8, 4, 22, 7, 6, 31, 7, 4, 6, 8, 3, 22, 5, 4, 8, 2, 5]
+EARLY = 2
+RECV_ROWS, N_SEND, N_RECV = 6400, 20, 112
+
+ORDER = [6, 7, 3, 5, 6, 8, 7, 3, 31, 0, 5, 4, 2, 6, 4, 8, 2, 22, 31, 7, 4, 8, 5, 6, 23, 22, 7, 5, 8, 6, 7, 8, 5, 6, 4,
+         7, 8, 5, 6, 30, 31, 6, 7, 8, 1, 4, 31, 0, 5, 6, 7, 8, 4, 6, 23, 5, 7, 8, 4, 6, 5, 21, 7, 30, 8, 6, 7, 5, 4,
+         20, 8, 1, 30, 6, 5, 8, 4, 30, 6, 7, 21, 20, 8, 4, 31, 6, 7, 5, 2, 30, 4, 8, 5, 3, 8]
 
 
 def split(x):
@@ -87,8 +87,8 @@
     def wait(self, rows, sem, narrow=False):
         self.descriptor(rows if narrow else 2 * rows, self.send_sem.at[0], sem).wait_recv()
 
-    def wait_sent(self, rows, sem):
-        self.descriptor(2 * rows, sem, self.recv_sem.at[0]).wait_send()
+    def wait_sent(self, rows, sem, narrow=False):
+        self.descriptor(rows if narrow else 2 * rows, sem, self.recv_sem.at[0]).wait_send()
 
     def drain(self):
         for sem, halves, when in self.sent.values():
@@ -119,9 +119,9 @@
 
     barrier = pltpu.get_barrier_semaphore()
     partners = [at_core(1 - core)]
-    partners += [at_z(lax.rem(z + d, NZ)) for d in range(1, NZ)]
-    partners += [at_y(lax.rem(y + d, NY)) for d in range(1, NY)]
-    partners += [at_x(lax.rem(x + d, NX)) for d in range(1, NX)]
+    partners += [at_z(lax.rem(z + d, NZ)) for d in (1, 2, NZ - 2, NZ - 1)]
+    partners += [at_y(lax.rem(y + d, NY)) for d in (1, NY - 1)]
+    partners += [at_x(lax.rem(x + d, NX)) for d in (1, NX - 1)]
     for partner in partners:
         pl.semaphore_signal(barrier, inc=1, device_id=(partner,), device_id_type=MESH)
 
@@ -231,45 +231,67 @@
         yield
         ex.wait(rows, sem)
 
-    def roots_sum(level, base, rows, count):
-        if count == 3:
-            places = [2 * r for r in range(3)]
-            is_root, my_root = jnp.logical_and(lax.rem(z, 2) == 0, z < 6), z // 2
-        else:
-            places = [r + r // 3 for r in range(6)]
-            is_root, my_root = lax.rem(z, 4) != 3, z - z // 4
-        not_root = jnp.logical_not(is_root)
-        first, sem, back = ex.slots((NZ - 1) * rows), ex.sem(), ex.sem()
-        for r, place in enumerate(places):
-            slot = jnp.maximum(lax.rem(z - place + NZ, NZ) - 1, 0)
-            ex.send(ex.at(part, level, base + r * rows, rows), ex.at(recv, None, first + slot * rows, rows),
-                    sem, at_z(place), (level, "in"), when=z != place, drain=False)
-        yield
-        where = base + jnp.where(is_root, my_root * rows, 0)
-
-        @pl.when(is_root)
+    def tree_sum(level, base, rows, narrow=False):
+        def role(d):
+            root = lax.rem(z - d + NZ, NZ)
+            return lax.rem(root, 4) != 3, root - root // 4
+
+        def block(ref, k):
+            if narrow:
+                return ex.at(ref, level, base + (k // 2) * rows, rows, lax.rem(k, 2) * 128)
+            return ex.at(ref, level, base + k * rows, rows)
+
+        def ahead(d):
+            return at_z(lax.rem(z + d + NZ, NZ))
+
+        def others(wait):
+            for there, count in ((lax.rem(z, 4) == 3, 4), (lax.rem(z, 4) == 1, 5), (lax.rem(z, 2) == 0, 3)):
+                pl.when(there)(functools.partial(wait, count * rows))
+
+        first = ex.slots(7 * rows)
+        slot = [ex.at(recv, None, first + k * rows, rows, 0 if narrow else None) for k in range(7)]
+        sem_below, sem_above, sem_root, back_below, back_above, back = [ex.sem() for _ in range(6)]
+        for d, to, k, sem in ((4, 2, 0, sem_below), (5, 1, 1, sem_below), (3, -1, 2, sem_above),
+                              (7, 1, 3, sem_root), (1, -1, 4, sem_root)):
+            there, mine_of = role(d)
+            ex.send(block(part, mine_of), slot[k], sem, ahead(to), (level, "others"), when=there, drain=False)
+        yield
+        for d, count, slots, sem, to, k in ((6, 2, (0, 1), sem_below, 2, 5), (2, 1, (2,), sem_above, -2, 6)):
+            there, mine_of = role(d)
+
+            @pl.when(there)
+            def _():
+                ex.wait(count * rows, sem, narrow)
+                total = block(part, mine_of)[...]
+                for slot_at in slots:
+                    total = total + slot[slot_at][...]
+                block(part, mine_of)[...] = total
+
+            ex.send(block(part, mine_of), slot[k], sem_root, ahead(to), (level, d), when=there)
+        yield
+        there, mine_of = role(0)
+
+        @pl.when(there)
         def _():
-            ex.wait((NZ - 1) * rows, sem)
-            total = part[level, pl.ds(aligned(where), rows), :]
-            for d in range(NZ - 1):
-                total = total + recv[pl.ds(first + d * rows, rows), :]
-            coef[level, pl.ds(aligned(where), rows), :] = total
-
-        block = ex.at(coef, level, where, rows)
-        for d in range(1, NZ):
-            ex.send(block, block, back, at_z(lax.rem(z + d, NZ)), (level, "out"), when=is_root)
-        yield
-        sent = ex.group((level, "in"))[0]
-
-        @pl.when(is_root)
-        def _():
-            ex.wait((count - 1) * rows, back)
-            ex.wait_sent((count - 1) * rows, sent)
-
-        @pl.when(not_root)
-        def _():
-            ex.wait(count * rows, back)
-            ex.wait_sent(count * rows, sent)
+            ex.wait(4 * rows, sem_root, narrow)
+            total = block(part, mine_of)[...]
+            for k in range(3, 7):
+                total = total + slot[k][...]
+            block(coef, mine_of)[...] = total
+
+        piece = block(coef, mine_of)
+        for to, sem in ((2, back_above), (-2, back_below), (1, back), (-1, back)):
+            ex.send(piece, piece, sem, ahead(to), (level, 0), when=there)
+        yield
+        for d, sem, targets in ((6, back_below, (-2, -1)), (2, back_above, (1,))):
+            there, mine_of = role(d)
+            pl.when(there)(functools.partial(ex.wait, rows, sem, narrow))
+            piece = block(coef, mine_of)
+            for to in targets:
+                ex.send(piece, piece, back, ahead(to), (level, d), when=there)
+        yield
+        others(lambda count: ex.wait(count, back, narrow))
+        others(lambda count: ex.wait_sent(count, ex.group((level, "others"))[0], narrow))
 
     def ring_blocks(level, base, rows, n, pos, narrow):
         def block(ref, lev, d, skip, size):
@@ -473,7 +495,7 @@
         yield from pair_in(7, mine, HALF // 2, bit, other)
         base, rows = mine + bit * (HALF // 2), HALF // 2 // NY
         yield from chain_in(7, base, rows, NY, y, at_y, part)
-        yield from roots_sum(7, base + y * rows, rows // 6, 6)
+        yield from tree_sum(7, base + y * rows, rows // 6)
         yield from chain_out(7, base, rows, NY, y, at_y)
         yield from pair_out(7, mine, HALF // 2, bit, other)
         yield from both_cores(7)
@@ -485,7 +507,7 @@
         yield from chain_in(8, mine, HALF // NX, NX, x, at_x, part)
         base, rows = mine + x * (HALF // NX), HALF // NX // NY
         yield from chain_in(8, base, rows, NY, y, at_y, part)
-        yield from roots_sum(8, base + y * rows, rows // 3, 3)
+        yield from tree_sum(8, base + y * rows, rows // 3, narrow=True)
         yield from chain_out(8, base, rows, NY, y, at_y)
         yield from chain_out(8, mine, HALF // NX, NX, x, at_x)
         yield from both_cores(8)

time: 69.3 us -> 66.8 us (0.964)
  Pallas kernels: 67.4 us -> 64.9 us
    pallas_call x1, Pallas kernels: 67.4 us -> 64.9 us  [body(): pl.pallas_call(kernel, out_shape=jax.ShapeDtypeStruct((V, R), F32), in_sp...]
where the time goes in v2:
time: 66.8 us; the launch traced here: 66.7 us
  Pallas kernels  64.9 us (97%)
  local copies, waits for them, and re-layouts  1.83 us (3%)
    pallas_call x1, Pallas kernels, body(): pl.pallas_call(kernel, out_shape=jax.ShapeDtypeStruct((V, R), F32), in_sp...  64.9 us
    unnamed x3, local copies, waits for them, and re-layouts  1.83 us

profile of v2, /device:TPU:1, one launch (start us, length us, event | category | flops | bytes accessed | tf_op | source)
XLA Modules:
  0.0 66.7 jit_solution(8479409157100955291)
XLA Ops:
  0.0 0.0 copy-start
  0.0 0.7 %copy-done = s32[512]{0:T(512)S(1)} copy-done((s32[512]{0:T(512)S(1)}, s32[512]{0:T(512)}, u32[]{:S(2)}) %copy-start) | copy-done | bytes 2072
  0.7 64.9 %coarse_solve.1 = f32[512,768]{1,0:T(8,128)S(1)} custom-call(f32[9,512,256]{2,1,0:T(8,128)} %basis.1, f32[512,768]{1,0:T(8,128)} %rhs.1, s32[1,512]{1,0:T(1,128)S(1)} %bitcast.1), custom_call_target="tpu_custom_call" | custom-call | tf_op jit(solution)/shard_map/coarse_solve/pallas_call | solution.py:535
  65.5 1.1 %copy.5 = f32[512,768]{1,0:T(8,128)} copy(f32[512,768]{1,0:T(8,128)S(1)} %coarse_solve.1) | data formatting | bytes 3145728
Async XLA Ops:
  0.0 0.7 %copy-start = (s32[512]{0:T(512)S(1)}, s32[512]{0:T(512)}, u32[]{:S(2)}) copy-start(s32[512]{0:T(512)} %param.5) | copy-start | bytes 6148

commit v3 on v2

--- a/solution.py
+++ b/solution.py
@@ -15,11 +15,11 @@
 NX, NY, NZ = 4, 4, 8
 LEVELS = 9
 EARLY = 2
-RECV_ROWS, N_SEND, N_RECV = 6400, 20, 112
-
-ORDER = [6, 7, 3, 5, 6, 8, 7, 3, 31, 0, 5, 4, 2, 6, 4, 8, 2, 22, 31, 7, 4, 8, 5, 6, 23, 22, 7, 5, 8, 6, 7, 8, 5, 6, 4,
-         7, 8, 5, 6, 30, 31, 6, 7, 8, 1, 4, 31, 0, 5, 6, 7, 8, 4, 6, 23, 5, 7, 8, 4, 6, 5, 21, 7, 30, 8, 6, 7, 5, 4,
-         20, 8, 1, 30, 6, 5, 8, 4, 30, 6, 7, 21, 20, 8, 4, 31, 6, 7, 5, 2, 30, 4, 8, 5, 3, 8]
+RECV_ROWS, N_SEND, N_RECV = 6400, 24, 112
+
+ORDER = [5, 3, 8, 6, 5, 3, 30, 8, 7, 2, 7, 6, 2, 21, 30, 4, 5, 1, 4, 22, 8, 6, 5, 7, 6, 31, 8, 7, 4, 1, 30, 6, 8, 0, 5,
+         0, 8, 7, 4, 5, 8, 7, 6, 4, 5, 8, 7, 6, 4, 5, 8, 6, 7, 4, 5, 8, 20, 31, 7, 4, 8, 5, 6, 30, 7, 8, 4, 21, 5, 23,
+         31, 7, 22, 4, 20, 6, 31, 8, 4, 23, 6, 5, 7, 30, 5, 31, 8, 2, 7, 3, 8]
 
 
 def split(x):
@@ -480,9 +480,7 @@
         project(6)
         yield from cores_in(6)
         yield from chain_in(6, mine, HALF // NY, NY, y, at_y, part)
-        base, rows = mine + y * (HALF // NY), HALF // NY // NZ * 2
-        yield from chain_in(6, base, rows, NZ, z, at_z, coef, narrow=True)
-        yield from chain_out(6, base, rows, NZ, z, at_z, narrow=True)
+        yield from tree_sum(6, mine + y * (HALF // NY), HALF // NY // 6)
         yield from chain_out(6, mine, HALF // NY, NY, y, at_y)
         yield from both_cores(6)
         apply(6, lambda rows: coef[6, rows])

time: 66.8 us -> 65.9 us (0.987)
  Pallas kernels: 64.9 us -> 64 us
    pallas_call x1, Pallas kernels: 64.9 us -> 64 us  [body(): pl.pallas_call(kernel, out_shape=jax.ShapeDtypeStruct((V, R), F32), in_sp...]
where the time goes in v3:
time: 65.9 us; the launch traced here: 65.8 us
  Pallas kernels  64 us (97%)
  local copies, waits for them, and re-layouts  1.83 us (3%)
    pallas_call x1, Pallas kernels, body(): pl.pallas_call(kernel, out_shape=jax.ShapeDtypeStruct((V, R), F32), in_sp...  64 us
    unnamed x3, local copies, waits for them, and re-layouts  1.83 us

profile of v3, /device:TPU:1, one launch (start us, length us, event | category | flops | bytes accessed | tf_op | source)
XLA Modules:
  0.0 65.8 jit_solution(816459165943130639)
XLA Ops:
  0.0 0.0 copy-start
  0.0 0.7 %copy-done = s32[512]{0:T(512)S(1)} copy-done((s32[512]{0:T(512)S(1)}, s32[512]{0:T(512)}, u32[]{:S(2)}) %copy-start) | copy-done | bytes 2072
  0.7 64.0 %coarse_solve.1 = f32[512,768]{1,0:T(8,128)S(1)} custom-call(f32[9,512,256]{2,1,0:T(8,128)} %basis.1, f32[512,768]{1,0:T(8,128)} %rhs.1, s32[1,512]{1,0:T(1,128)S(1)} %bitcast.1), custom_call_target="tpu_custom_call" | custom-call | tf_op jit(solution)/shard_map/coarse_solve/pallas_call | solution.py:533
  64.7 1.1 %copy.5 = f32[512,768]{1,0:T(8,128)} copy(f32[512,768]{1,0:T(8,128)S(1)} %coarse_solve.1) | data formatting | bytes 3145728
Async XLA Ops:
  0.0 0.7 %copy-start = (s32[512]{0:T(512)S(1)}, s32[512]{0:T(512)}, u32[]{:S(2)}) copy-start(s32[512]{0:T(512)} %param.5) | copy-start | bytes 6148
